TPU v7x, 32 devices: a whole 2x2x4 slice. The times are simulated.
32 devices in a mesh: freq: 8 (over z, x), sens: 4 (over y, core).
Axes of the slice: x: 2, y: 2, z: 4, core: 2. Of those that a mesh axis runs over, the one named last changes fastest.
Arguments:
- samples: bfloat16 [128, 608, 420], P('freq', 'sens'), may hold values from -6 to 6
- response_tiles: bfloat16 [448, 2, 608, 21], P('freq', None, 'sens'), may hold values from -0.25 to 0.25
- slot_sensor: int32 [608], P('sens'), may hold values from -1 to 599, as said below
- sensor_noise: float32 [600], replicated, may hold values from 0.02 to 5
- advance_offset: int32 [21], replicated, may hold values from 0 to 419
Outputs:
- outlook_values: bfloat16 [128, 21, 420], P('freq')
- noise_spread: float32 [21], replicated
Inputs may be any that keep to these rules, and one draw needn't show every extreme that they name: `slot_sensor`: every sensor number appears in exactly one slot; the other 8 slots hold -1.
All inputs are finite; a program needn't handle non-finite values.
Results may differ from a plain program's by a relative error of at most 0.0055.
Values may be sent and summed in bfloat16 or wider, within the bound.
A program may use at most 64 MiB of HBM per device.

v0:
```python
import functools
import math

import jax
import jax.numpy as jnp
import numpy as np
from jax import lax
from jax.experimental import pallas as pl
from jax.experimental.pallas import tpu as pltpu
from jax.sharding import PartitionSpec as P

MESH = pl.DeviceIdType.MESH
HALF = 64
LANES = 128


def make_tables(freq_size, bins_dev, step_count, group, chunks):
    bin_count = freq_size * bins_dev
    period = 2 * bin_count
    slot = np.arange(freq_size * chunks * group)
    block, inside = slot // (chunks * group), slot % (chunks * group)
    live = (inside < bins_dev).astype(np.float64)
    bins = np.where(inside < bins_dev, block * bins_dev + inside, 0)
    turns = bins[:, None] * np.arange(step_count)[None, :] % period
    angle = turns * (2.0 * math.pi / period)
    forward = np.stack([np.cos(angle), -np.sin(angle)]) * live[None, :, None]
    weight = np.where(bins == 0, 1.0, 2.0) / period * live
    inverse = np.stack([np.cos(angle), -np.sin(angle)]) * weight[None, :, None]
    inverse = inverse.reshape(2, freq_size * chunks, group, step_count).transpose(0, 2, 1, 3)
    inverse = inverse.reshape(2 * group * freq_size * chunks, step_count)
    return bins, weight, forward, inverse


def kernel(
    dims,
    tiles, samples_in, forward_in, slot_ids, sensor_noise, sorter, noise_weight, bins, offsets, inverse_in,
    out, spread, samples, forward, inverse, slot_facts, cosine, sine, load_sem,
    held, spectra, z_own, z_send, z_recv, gathered, spread_send, spread_recv,
    ring_send, ring_recv, z_send_sem, z_recv_sem, s_send_sem, s_recv_sem,
):
    freq_size, sens_size, chunks, group, sites, count, period_of = dims
    rows, slots, step_count = samples_in.shape
    all_chunks = freq_size * chunks
    per_bin = 2 * rows
    lane_tiles = spectra.shape[0]
    me_f = lax.axis_index("freq")
    me_s = lax.axis_index("sens")
    n = freq_size

    def position_of(index):
        odd, pair = lax.rem(index, 2), index // 2
        return pair * (1 - odd) + (n - 1 - pair) * odd

    def index_of(position):
        high = position // (n // 2)
        return 2 * position * (1 - high) + (2 * (n - 1 - position) + 1) * high

    me_p = position_of(me_f)

    def along(step):
        return index_of(lax.rem(me_p + step + 2 * n, n))

    right, left = along(1), along(-1)
    barrier = pltpu.get_barrier_semaphore()
    for neighbour in (left, right):
        pl.semaphore_signal(barrier, inc=1, device_id={"freq": neighbour}, device_id_type=MESH)
    for d in range(1, sens_size):
        peer = lax.rem(me_s + d, sens_size)
        pl.semaphore_signal(barrier, inc=1, device_id={"sens": peer}, device_id_type=MESH)

    cuts = [chunks * i // count for i in range(count + 1)]
    cuts = [cut + cut % 2 for cut in cuts[:-1]] + [chunks]
    edges = [cut * slots for cut in cuts[:-1]] + [held.shape[1]]
    half = count // 2
    pieces = [j for i in range(half) for j in (i, half + i) if cuts[j + 1] > cuts[j]]
    sign_of = (1,) * half + (-1,) * half

    def ring_copy(step, j, received):
        d = sign_of[j]
        low, size = edges[j], edges[j + 1] - edges[j]
        origin = along(-d * (step + (1 if received else 0)))
        block = held.at[origin, pl.ds(low, size)]
        return pltpu.make_async_remote_copy(
            src_ref=block, dst_ref=block,
            send_sem=ring_send.at[j, step], recv_sem=ring_recv.at[j, step],
            device_id={"freq": right if d == 1 else left}, device_id_type=MESH,
        )

    loads = [
        pltpu.make_async_copy(source, target, load_sem.at[at])
        for at, (source, target) in enumerate(
            ((forward_in, forward), (samples_in, samples), (inverse_in, inverse))
        )
    ]
    for load in loads:
        load.start()
    ids = slot_ids[...]
    same = ids == lax.broadcasted_iota(jnp.int32, (slots, sensor_noise.shape[1]), 1)
    found = jnp.sum(jnp.where(same, sensor_noise[...], 0.0), axis=1, keepdims=True)
    slot_facts[0] = jnp.broadcast_to(found, (slots, LANES))
    slot_facts[1] = jnp.broadcast_to((ids >= 0).astype(jnp.float32), (slots, LANES))
    width = group * 2 * sites

    def sort_tiles(j):
        for chunk in range(cuts[j], cuts[j + 1]):
            low = chunk * width
            size = min(width, tiles.shape[0] - low)
            turned = lax.dot_general(
                tiles[low:low + size, :], sorter[:size, :], (((0,), (0,)), ((), ())),
                preferred_element_type=jnp.float32,
            )
            held[me_f, chunk * slots:(chunk + 1) * slots] = jnp.where(slot_facts[1] > 0.5, turned, 0.0).astype(jnp.bfloat16)

    for at, j in enumerate(pieces):
        sort_tiles(j)
        if at == 0:
            pl.semaphore_wait(barrier, 2 + sens_size - 1)
        else:
            ring_copy(0, pieces[at - 1], False).start()

    lane = lax.broadcasted_iota(jnp.int32, (rows, LANES), 1)
    which = (lane % HALF) // sites
    sign = jnp.where(lane < HALF, -1.0, 1.0).astype(jnp.float32)
    spread[...] = jnp.zeros_like(spread)

    def transform(r):
        for c in range(2):
            value = lax.dot_general(
                forward[c], samples[r], (((1,), (1,)), ((), ())),
                preferred_element_type=jnp.float32,
            )
            for tile in range(lane_tiles):
                part = value[:, tile * LANES:min(slots, (tile + 1) * LANES)]
                if part.shape[1] < LANES:
                    part = jnp.concatenate(
                        [part, jnp.zeros((part.shape[0], LANES - part.shape[1]), part.dtype)], axis=1
                    )
                spectra[tile, pl.ds(c * rows + r, part.shape[0], stride=per_bin), :] = part

    def contract(step, j):
        origin = along(-sign_of[j] * step)
        for chunk in range(cuts[j], cuts[j + 1]):
            at = origin * chunks + chunk
            weights = held[origin, chunk * slots:(chunk + 1) * slots]
            first = pl.multiple_of(at * (group * per_bin), group * per_bin)
            parts = [spectra[tile, pl.ds(first, group * per_bin), :] for tile in range(lane_tiles)]
            spec = jnp.concatenate(parts, axis=1)[:, :slots].astype(jnp.bfloat16)
            product = jnp.dot(spec, weights, preferred_element_type=jnp.float32)
            picked = [product[c * rows:(c + 1) * rows] for c in range(2)]
            for i in range(1, group):
                for c in range(2):
                    low = i * per_bin + c * rows
                    picked[c] = jnp.where(which == i, product[low:low + rows], picked[c])
            value = picked[0] + sign * pltpu.roll(picked[1], HALF, 1)
            z_own[pl.ds(pl.multiple_of(at * rows, rows), rows), :] = value
            z_send[at] = value.astype(jnp.bfloat16)
            wide = weights.astype(jnp.float32)
            power = wide * wide * slot_facts[0]
            total = power.reshape(slots // 8, 8, LANES).sum(axis=0)
            spread[...] += total * noise_weight[pl.ds(at, 1), :]

    def z_copies(step, j):
        origin = along(-sign_of[j] * step)
        part = pl.ds(origin * chunks + cuts[j], cuts[j + 1] - cuts[j])
        return [
            pltpu.make_async_remote_copy(
                src_ref=z_send.at[part], dst_ref=z_recv.at[d - 1, part],
                send_sem=z_send_sem.at[d - 1, step * count + j],
                recv_sem=z_recv_sem.at[d - 1, step * count + j],
                device_id={"sens": lax.rem(me_s + d, sens_size)}, device_id_type=MESH,
            )
            for d in range(1, sens_size)
        ]

    def receive(step, j, last):
        ring_copy(step, j, True).wait_recv()
        if not last:
            ring_copy(step + 1, j, False).start()

    def send_z(step, j):
        for copy in z_copies(step, j):
            copy.start()

    def transforms(low, high):
        lax.fori_loop(low, high, lambda r, carry: (transform(r), carry)[1], 0)

    ring_copy(0, pieces[-1], False).start()
    period = float(period_of)
    ahead = bins[...] * offsets[...]
    angle = (ahead - period * jnp.floor(ahead / period)) * (2.0 * math.pi / period)
    side = lax.broadcasted_iota(jnp.int32, angle.shape, 1)
    cosine[...] = jnp.cos(angle)
    sine[...] = jnp.sin(angle) * jnp.where(side < HALF, -1.0, 1.0)
    for load in loads:
        load.wait()
    turns = 2 * len(pieces)
    done = 0
    for turn in range(turns):
        receive(turn // len(pieces), pieces[turn % len(pieces)], False)
        upto = rows * (turn + 1) // turns
        transforms(done, upto)
        done = upto

    def both(step, carry):
        for at, j in enumerate(pieces):
            receive(step, j, False)

            def one(arrival, inner):
                contract(arrival, j)
                return inner

            lax.fori_loop(2 * (step - 2), 2 * (step - 2) + 2, one, 0)
            for arrival in (2 * (step - 2), 2 * (step - 2) + 1):
                if at > 0:
                    send_z(arrival, pieces[at - 1])
                if at == len(pieces) - 1:
                    send_z(arrival, j)
        return carry

    lax.fori_loop(2, 5, both, 0)

    def single(step, carry):
        for at, j in enumerate(pieces):
            ring_copy(step, j, True).wait_recv()

            @pl.when(step < n - 2)
            def _():
                ring_copy(step + 1, j, False).start()

            contract(step + 1, j)
            if at > 0:
                send_z(step + 1, pieces[at - 1])
            if at == len(pieces) - 1:
                send_z(step + 1, j)
        return carry

    lax.fori_loop(5, n - 1, single, 0)
    spread_send[...] = spread[...]
    spread_copies = [
        pltpu.make_async_remote_copy(
            src_ref=spread_send, dst_ref=spread_recv.at[d - 1],
            send_sem=s_send_sem.at[d - 1], recv_sem=s_recv_sem.at[d - 1],
            device_id={"sens": lax.rem(me_s + d, sens_size)}, device_id_type=MESH,
        )
        for d in range(1, sens_size)
    ]
    for copy in spread_copies:
        copy.start()
    for step in range(n - 1):
        for j in pieces:
            ring_copy(step, j, False).wait_send()
    for step in range(n):
        for j in pieces:
            for copy in z_copies(step, j):
                copy.wait()
    for copy in spread_copies:
        copy.wait()
    total = spread[...]
    for d in range(1, sens_size):
        total += spread_recv[d - 1]
    total = jnp.broadcast_to(jnp.sum(total, axis=0, keepdims=True), total.shape)
    total = total + pltpu.roll(total, HALF, 1)
    folded = total
    for i in range(1, group):
        folded += pltpu.roll(total, LANES - i * sites, 1)
    spread[...] = folded

    def combine(at, carry):
        here = pl.ds(pl.multiple_of(at * rows, rows), rows)
        value = z_own[here, :]
        for d in range(1, sens_size):
            value += z_recv[d - 1, at].astype(jnp.float32)
        z_own[here, :] = value * cosine[pl.ds(at, 1), :] + pltpu.roll(value, HALF, 1) * sine[pl.ds(at, 1), :]
        return carry

    lax.fori_loop(0, all_chunks, combine, 0, unroll=4)

    seat = 32
    together = LANES // seat
    place = lax.broadcasted_iota(jnp.int32, (all_chunks, LANES), 1) // seat
    for base in range(0, rows, together):
        mine = [z_own[pl.ds(base + m, all_chunks, stride=rows), :] for m in range(together)]
        for c in range(2):
            for i in range(group):
                start = c * HALF + i * sites
                value = None
                for m in range(together):
                    moved = pltpu.roll(mine[m], (m * seat - start) % LANES, 1)
                    value = moved if value is None else jnp.where(place == m, moved, value)
                low = (c * group + i) * all_chunks
                gathered[low:low + all_chunks, base * seat:(base + together) * seat] = value.astype(jnp.bfloat16)
    result = lax.dot_general(
        gathered[...], inverse[...], (((0,), (0,)), ((), ())), preferred_element_type=jnp.float32
    )
    for r in range(rows):
        out[r] = result[r * seat:r * seat + sites].astype(jnp.bfloat16)


def on_device(freq_size, sens_size, samples, response_tiles, slot_sensor, sensor_noise, advance_offset):
    bins_dev, _, slots, sites = response_tiles.shape
    rows, _, step_count = samples.shape
    group = HALF // sites
    chunks = -(-bins_dev // group)
    all_chunks = freq_size * chunks
    period = 2 * freq_size * bins_dev
    bins, weight, forward, inverse = make_tables(freq_size, bins_dev, step_count, group, chunks)

    def per_lane(table):
        table = table.reshape(all_chunks, group * sites)
        table = np.pad(table, ((0, 0), (0, HALF - group * sites)))
        return jnp.asarray(np.concatenate([table, table], axis=1))

    tiles = response_tiles.transpose(0, 3, 1, 2).reshape(bins_dev * 2 * sites, slots)
    sorter = np.zeros((group, sites, 2, LANES), np.float32)
    for i, q, c in np.ndindex(group, sites, 2):
        sorter[i, q, c, c * HALF + i * sites + q] = 1.0
    sorter = jnp.asarray(sorter.reshape(group * sites * 2, LANES), jnp.bfloat16)

    offsets = jnp.tile(advance_offset.astype(jnp.float32), group)
    offsets = jnp.tile(jnp.pad(offsets, (0, HALF - group * sites)), 2)[None, :]
    lane_bins = per_lane(np.repeat(bins[:, None], sites, axis=1).astype(np.float32))
    noise_weight = per_lane(np.repeat(weight[:, None], sites, axis=1).astype(np.float32))

    lane_tiles = -(-slots // LANES)
    peers = sens_size - 1
    count = 4 if peers * freq_size * 4 <= 1024 else 2
    vmem = pl.BlockSpec(memory_space=pltpu.VMEM)
    anywhere = pl.BlockSpec(memory_space=pl.ANY)
    outlook, spread = pl.pallas_call(
        functools.partial(kernel, (freq_size, sens_size, chunks, group, sites, count, period)),
        out_shape=(
            jax.ShapeDtypeStruct((rows, sites, step_count), jnp.bfloat16),
            jax.ShapeDtypeStruct((8, LANES), jnp.float32),
        ),
        in_specs=[vmem, anywhere, anywhere] + [vmem] * 6 + [anywhere],
        out_specs=(vmem, vmem),
        scratch_shapes=[
            pltpu.VMEM(samples.shape, jnp.bfloat16),
            pltpu.VMEM(forward.shape, jnp.bfloat16),
            pltpu.VMEM(inverse.shape, jnp.bfloat16),
            pltpu.VMEM((2, slots, LANES), jnp.float32),
            pltpu.VMEM((all_chunks, LANES), jnp.float32),
            pltpu.VMEM((all_chunks, LANES), jnp.float32),
            pltpu.SemaphoreType.DMA((3,)),
            pltpu.VMEM((freq_size, -(-chunks * slots // 16) * 16, LANES), jnp.bfloat16),
            pltpu.VMEM((lane_tiles, all_chunks * group * 2 * rows, LANES), jnp.float32),
            pltpu.VMEM((all_chunks * rows, LANES), jnp.float32),
            pltpu.VMEM((all_chunks, rows, LANES), jnp.bfloat16),
            pltpu.VMEM((peers, all_chunks, rows, LANES), jnp.bfloat16),
            pltpu.VMEM((2 * group * all_chunks, rows * 32), jnp.bfloat16),
            pltpu.VMEM((8, LANES), jnp.float32),
            pltpu.VMEM((peers, 8, LANES), jnp.float32),
            pltpu.SemaphoreType.DMA((count, freq_size - 1)),
            pltpu.SemaphoreType.DMA((count, freq_size - 1)),
            pltpu.SemaphoreType.DMA((peers, freq_size * count)),
            pltpu.SemaphoreType.DMA((peers, freq_size * count)),
            pltpu.SemaphoreType.DMA((peers,)),
            pltpu.SemaphoreType.DMA((peers,)),
        ],
        compiler_params=pltpu.CompilerParams(
            collective_id=0, has_side_effects=True, vmem_limit_bytes=60 * 1024 * 1024
        ),
    )(
        tiles, samples, jnp.asarray(forward, jnp.bfloat16), slot_sensor[:, None], sensor_noise[None, :],
        sorter, noise_weight, lane_bins, offsets, jnp.asarray(inverse, jnp.bfloat16),
    )
    noise_spread = spread[0, :sites]
    return (outlook, noise_spread)


def solution(mesh):
    placed = (P("freq", "sens", None), P("freq", None, "sens", None), P("sens"), P(), P())
    return jax.shard_map(
        functools.partial(on_device, mesh.shape["freq"], mesh.shape["sens"]),
        mesh=mesh,
        in_specs=placed,
        out_specs=(P("freq", None, None), P()),
        check_vma=False,
    )
```

profile of v0, /device:TPU:0, one launch (start us, length us, event | category | flops | bytes accessed | tf_op | source)
XLA Modules:
  0.0 89.5 jit_solution(11717600767402394292)
XLA Ops:
  0.6 0.7 convert_element_type.5
  1.3 0.1 tile.7
  1.4 0.6 broadcast_in_dim_tile.3.offsets
  2.0 1.3 %broadcast_in_dim.7.sensor_noise = f32[1,600]{1,0:T(1,128)} reshape(f32[600]{0:T(1024)} %param.13) | data formatting | bytes 4800 | tf_op jit(solution)/shard_map/broadcast_in_dim | solution.py:364
  3.3 1.4 %copy.13.slot_ids = s32[152,1]{1,0:T(8,128)} copy(s32[152,1]{0,1:T(1,128)} %bitcast.5) | data formatting | bytes 1216 | tf_op jit(solution)/shard_map/broadcast_in_dim | solution.py:364
  4.7 3.8 %reshape.9.tiles = bf16[2352,152]{1,0:T(8,128)(2,1)} reshape(bf16[56,21,2,152]{3,2,1,0:T(2,128)(2,1)} %bitcast.4) | data formatting | bytes 1430016 | tf_op jit(solution)/shard_map/reshape | solution.py:313
  8.5 77.9 %shard_map.113 = (bf16[16,21,420]{2,1,0:T(8,128)(2,1)}, f32[8,128]{1,0:T(8,128)}) custom-call(bf16[2352,152]{1,0:T(8,128)(2,1)} %reshape.9.tiles, bf16[16,152,420]{2,1,0:T(8,128)(2,1)} %samples_in.1, bf16[2,456,420]{2,1,0:T(8,128)(2,1)} %constant.16.clone.forward_in, s32[152,1]{1,0:T(8,128)} %copy.13.slot_ids, f32[1,600]{1,0:T(1,128)} %broadcast_in_dim.7.sensor_noise, ...), custom_call_target="tpu_custom_call" | custom-call | tf_op jit(solution)/shard_map/pallas_call | solution.py:329
  86.5 1.8 %copy.14 = bf16[16,21,420]{2,0,1:T(8,128)(2,1)} copy(bf16[16,21,420]{2,1,0:T(8,128)(2,1)} %get-tuple-element.8) | data formatting | bytes 564480
  88.3 1.2 %slice_bitcast_fusion = f32[21]{0:T(128)} fusion(f32[8,128]{1,0:T(8,128)} %get-tuple-element.5), kind=kLoop, calls=%fused_computation | loop fusion | bytes 168 | tf_op jit(solution)/shard_map/squeeze | solution.py:367
  (3 shorter events, 0.0 us)
where the time goes:
time: 89.8 us; the launch traced here: 89.5 us
  Pallas kernels  77.9 us (87%)
  local copies, waits for them, and re-layouts  10.3 us (11%)
    pallas_call x1, Pallas kernels, on_device(): pl.pallas_call(functools.partial(kernel, (freq_size, sens_size, chunks, g...  77.9 us
    reshape x1, local copies, waits for them, and re-layouts, on_device(): response_tiles.transpose(0, 3, 1, 2).reshape(bins_dev * 2 * sites, slots)  3.84 us
    unnamed x1, local copies, waits for them, and re-layouts  1.84 us

commit v1 on v0

v1 whole, which is shorter than its diff:
```python
import functools
import math

import jax
import jax.numpy as jnp
import numpy as np
from jax import lax
from jax.experimental import pallas as pl
from jax.experimental.pallas import tpu as pltpu
from jax.sharding import PartitionSpec as P

MESH = pl.DeviceIdType.MESH
HALF = 64
LANES = 128
SEAT = 32


class Plan:
    def __init__(self, bins_dev, slots, sites, halves):
        self.bins_dev, self.slots, self.sites = bins_dev, slots, sites
        self.group = HALF // sites
        self.chunks = -(-bins_dev // self.group)
        full = self.chunks // 2
        cut = -(-slots // 32) * 16
        plus = [(c, 0, slots) for c in range(full)]
        minus = [(c, 0, slots) for c in range(self.chunks - full, self.chunks)]
        if self.chunks % 2:
            plus.append((full, 0, cut))
            minus.append((full, cut, slots))
        self.parts = (plus, minus)
        self.m = len(plus)
        self.pad = -(-self.m // 16) * 16
        self.rows = [sum(hi - lo for _, lo, hi in part) for part in self.parts]
        self.held_rows = -(-max(self.rows) // 16) * 16
        ends = [-(-self.m * h // halves) for h in range(halves + 1)]
        self.halves = halves
        self.spans = list(zip(ends[:-1], ends[1:]))
        self.pieces = [(d, h) for h in range(halves) for d in range(2)]

    def size(self, chunk):
        return min(self.group, self.bins_dev - chunk * self.group)

    def row(self, d, k):
        return sum(hi - lo for _, lo, hi in self.parts[d][:k])


def make_tables(freq_size, plan, step_count):
    bins_dev, group, chunks = plan.bins_dev, plan.group, plan.chunks
    period = 2 * freq_size * bins_dev
    slot = np.arange(freq_size * chunks * group)
    block, inside = slot // (chunks * group), slot % (chunks * group)
    live = (inside < bins_dev).astype(np.float64)
    bins = np.where(inside < bins_dev, block * bins_dev + inside, 0)
    turns = bins[:, None] * np.arange(step_count)[None, :] % period
    angle = turns * (2.0 * math.pi / period)
    forward = np.stack([np.cos(angle), -np.sin(angle)]) * live[None, :, None]
    inverse = np.zeros((freq_size, 2, group, 2, plan.pad, step_count))
    weight = (np.where(bins == 0, 1.0, 2.0) / period).reshape(freq_size, chunks, group)
    table = forward.reshape(2, freq_size, chunks, group, step_count) * weight[None, ..., None]
    for d in range(2):
        for k, (chunk, _, _) in enumerate(plan.parts[d]):
            inverse[:, :, :, d, k] = table[:, :, chunk].transpose(1, 0, 2, 3)
    return forward, inverse.reshape(freq_size, 4 * group * plan.pad, step_count)


def kernel(
    freq_size, sens_size, plan,
    tiles_in, samples_in, forward_in, inverse_in, slots_in, noise_in, offsets_in,
    out, spread_out,
    raw, samples, forward, inverse, ids, noise, offsets, load_sem, tile_sem,
    facts, live, cosine, sine, weight,
    held, spectra, z_own, z_send, z_recv, turned_z, gathered, total, spread, spread_send, spread_recv,
    ring_send, ring_recv, z_send_sem, z_recv_sem, s_send_sem, s_recv_sem,
):
    rows, slots, step_count = samples.shape
    n, group, chunks, sites, m, pad = freq_size, plan.group, plan.chunks, plan.sites, plan.m, plan.pad
    bins_dev = plan.bins_dev
    per_bin = 2 * rows
    lane_tiles = spectra.shape[0]
    period = 2 * n * bins_dev
    pieces, halves = plan.pieces, plan.halves
    me_f = lax.axis_index("freq")
    me_s = lax.axis_index("sens")

    def position_of(index):
        odd, pair = lax.rem(index, 2), index // 2
        return pair * (1 - odd) + (n - 1 - pair) * odd

    def index_of(position):
        high = position // (n // 2)
        return 2 * position * (1 - high) + (2 * (n - 1 - position) + 1) * high

    me_p = position_of(me_f)

    def along(step):
        return index_of(lax.rem(me_p + step + 2 * n, n))

    def origin_of(d, arrival):
        return along(arrival if d else -arrival)

    right, left = along(1), along(-1)
    barrier = pltpu.get_barrier_semaphore()
    for neighbour in (left, right):
        pl.semaphore_signal(barrier, inc=1, device_id={"freq": neighbour}, device_id_type=MESH)
    for d in range(1, sens_size):
        peer = lax.rem(me_s + d, sens_size)
        pl.semaphore_signal(barrier, inc=1, device_id={"sens": peer}, device_id_type=MESH)

    tile_loads = []
    for at, (d, h) in enumerate(pieces):
        needed = [
            chunk for chunk, low, high in plan.parts[d][slice(*plan.spans[h])]
            if d == 0 or high - low == slots
        ]
        if needed:
            low = needed[0] * group
            span = pl.ds(low, min((needed[-1] + 1) * group, bins_dev) - low)
            tile_loads.append([pltpu.make_async_copy(tiles_in.at[span], raw.at[span], tile_sem.at[at])])
        else:
            tile_loads.append([])
    loads = [
        pltpu.make_async_copy(source, target, load_sem.at[at])
        for at, (source, target) in enumerate((
            (slots_in, ids), (noise_in, noise), (offsets_in, offsets),
            (forward_in, forward), (samples_in, samples), (inverse_in, inverse),
        ))
    ]
    for load in sum(tile_loads, []) + loads:
        load.start()

    def ring_copy(step, piece, received):
        d, h = piece
        low, high = (plan.row(d, k) for k in plan.spans[h])
        origin = origin_of(d, step + (1 if received else 0))
        block = held.at[d, origin, pl.ds(low, high - low)]
        at = 2 * h + d
        return pltpu.make_async_remote_copy(
            src_ref=block, dst_ref=block,
            send_sem=ring_send.at[at, step], recv_sem=ring_recv.at[at, step],
            device_id={"freq": left if d else right}, device_id_type=MESH,
        )

    line = lax.broadcasted_iota(jnp.int32, (group * sites * 2, LANES), 0)
    spot = lax.broadcasted_iota(jnp.int32, (group * sites * 2, LANES), 1)
    sorter = (spot == lax.rem(line, 2) * HALF + line // 2).astype(jnp.float32).astype(jnp.bfloat16)

    def sort_tiles(d, h):
        for k in range(*plan.spans[h]):
            chunk, low, high = plan.parts[d][k]
            whole = (low, high) == (0, slots)
            if d and not whole:
                continue
            size = plan.size(chunk)
            block = raw[chunk * group:chunk * group + size].reshape(size * sites * 2, slots)
            turned = lax.dot_general(
                block, sorter[:size * sites * 2], (((0,), (0,)), ((), ())),
                preferred_element_type=jnp.float32,
            ).astype(jnp.bfloat16)
            at = plan.row(d, k)
            held[d, me_f, at:at + high - low] = turned[low:high]
            if not whole:
                at = plan.row(1, m - 1)
                held[1, me_f, at:at + slots - high] = turned[high:]

    for at, piece in enumerate(pieces):
        for load in tile_loads[at]:
            load.wait()
        sort_tiles(*piece)
        if at == 0:
            pl.semaphore_wait(barrier, 2 + sens_size - 1)
        ring_copy(0, piece, False).start()

    for load in loads[:3]:
        load.wait()

    def fact(s, carry):
        sensor = ids[s]
        there = (sensor >= 0).astype(jnp.float32)
        facts[0, pl.ds(s, 1), :] = jnp.full((1, LANES), noise[jnp.maximum(sensor, 0)] * there)
        facts[1, pl.ds(s, 1), :] = jnp.full((1, LANES), there)
        return carry

    lax.fori_loop(0, slots, fact, 0, unroll=8)
    there = facts[1].astype(jnp.bfloat16)
    live[...] = jnp.concatenate([there] * (live.shape[1] // LANES), axis=1)
    spread[...] = jnp.zeros_like(spread)
    turned_z[...] = jnp.zeros_like(turned_z)
    total[...] = jnp.zeros_like(total)

    lane = lax.broadcasted_iota(jnp.int32, (rows, LANES), 1)
    which = (lane % HALF) // sites
    sign = jnp.where(lane < HALF, -1.0, 1.0).astype(jnp.float32)

    place = lax.broadcasted_iota(jnp.int32, (2 * pad, LANES), 1)
    seat = lax.broadcasted_iota(jnp.int32, (2 * pad, LANES), 0)
    inside = place % HALF
    lead = jnp.zeros((2 * pad, LANES), jnp.float32)
    for q in range(sites):
        lead = jnp.where(inside % sites == q, offsets[q].astype(jnp.float32), lead)
    side = seat // pad
    chunk_of = jnp.zeros_like(seat)
    for d in range(2):
        for k in range(m):
            chunk_of = jnp.where(seat == d * pad + k, plan.parts[d][k][0], chunk_of)
    within = chunk_of * group + inside // sites
    alive = (within < bins_dev) & (inside < group * sites) & (seat % pad < m)
    turning = 2.0 * math.pi / period

    def phase(arrival, carry):
        block = jnp.where(side == 0, origin_of(0, arrival), origin_of(1, arrival))
        bins = block * bins_dev + within
        ahead = bins.astype(jnp.float32) * lead
        angle = (ahead - period * jnp.floor(ahead / period)) * turning
        here = pl.ds(pl.multiple_of(arrival * 2 * pad, 2 * pad), 2 * pad)
        cosine[here, :] = jnp.cos(angle)
        sine[here, :] = jnp.sin(angle) * jnp.where(place < HALF, -1.0, 1.0)
        weight[here, :] = jnp.where(alive, jnp.where(bins == 0, 1.0, 2.0) / period, 0.0)
        return carry

    lax.fori_loop(0, n, phase, 0)

    def transform(r):
        sample = samples[r] * live[:, :step_count]
        for c in range(2):
            value = lax.dot_general(
                forward[c], sample, (((1,), (1,)), ((), ())),
                preferred_element_type=jnp.float32,
            )
            for tile in range(lane_tiles):
                part = value[:, tile * LANES:min(slots, (tile + 1) * LANES)]
                if part.shape[1] < LANES:
                    part = jnp.concatenate(
                        [part, jnp.zeros((part.shape[0], LANES - part.shape[1]), part.dtype)], axis=1
                    )
                spectra[tile, pl.ds(c * rows + r, part.shape[0], stride=per_bin), :] = part

    def transforms(low, high):
        lax.fori_loop(low, high, lambda r, carry: (transform(r), carry)[1], 0)

    def z_row(arrival, d, k):
        return (arrival * 2 + d) * m + k

    def contract(arrival, piece):
        d, h = piece
        origin = origin_of(d, arrival)
        noisy = spread[...]
        for k in range(*plan.spans[h]):
            chunk, low, high = plan.parts[d][k]
            row = plan.row(d, k)
            weights = held[d, origin, row:row + high - low]
            first = pl.multiple_of((origin * chunks + chunk) * (group * per_bin), group * per_bin)
            parts = [spectra[tile, pl.ds(first, group * per_bin), :] for tile in range(lane_tiles)]
            spec = jnp.concatenate(parts, axis=1)[:, :slots].astype(jnp.bfloat16)
            filled = weights
            if high - low < slots:
                filled = jnp.concatenate(
                    ([jnp.zeros((low, LANES), jnp.bfloat16)] if low else []) + [weights]
                    + ([jnp.zeros((slots - high, LANES), jnp.bfloat16)] if high < slots else []), axis=0
                )
            product = jnp.dot(spec, filled, preferred_element_type=jnp.float32)
            picked = [product[c * rows:(c + 1) * rows] for c in range(2)]
            for i in range(1, group):
                for c in range(2):
                    at = i * per_bin + c * rows
                    picked[c] = jnp.where(which == i, product[at:at + rows], picked[c])
            value = picked[0] + sign * pltpu.roll(picked[1], HALF, 1)
            at = z_row(arrival, d, k)
            z_own[pl.ds(pl.multiple_of(at * rows, rows), rows), :] = value
            z_send[at] = value.astype(jnp.bfloat16)
            wide = weights.astype(jnp.float32)
            power = wide * wide * facts[0, low:high]
            power = power.reshape((high - low) // 8, 8, LANES).sum(axis=0)
            noisy += power * weight[pl.ds(arrival * 2 * pad + d * pad + k, 1), :]
        spread[...] = noisy

    def z_copies(arrival, piece):
        d, h = piece
        low, high = plan.spans[h]
        part = pl.ds(z_row(arrival, d, low), high - low)
        at = arrival * len(pieces) + 2 * h + d
        return [
            pltpu.make_async_remote_copy(
                src_ref=z_send.at[part], dst_ref=z_recv.at[p - 1, part],
                send_sem=z_send_sem.at[p - 1, at], recv_sem=z_recv_sem.at[p - 1, at],
                device_id={"sens": lax.rem(me_s + p, sens_size)}, device_id_type=MESH,
            )
            for p in range(1, sens_size)
        ]

    def send_z(arrival, piece):
        for copy in z_copies(arrival, piece):
            copy.start()

    def receive(step, piece, last=False):
        ring_copy(step, piece, True).wait_recv()
        if not last:
            ring_copy(step + 1, piece, False).start()

    together = LANES // SEAT
    seat_of = lax.broadcasted_iota(jnp.int32, (pad, LANES), 1) // SEAT

    def finish(arrival):
        for piece in pieces:
            for copy in z_copies(arrival, piece):
                copy.wait_recv()
        for d in range(2):
            for k in range(m):
                at = z_row(arrival, d, k)
                value = z_own[pl.ds(pl.multiple_of(at * rows, rows), rows), :]
                for p in range(1, sens_size):
                    value += z_recv[p - 1, at].astype(jnp.float32)
                near = pl.ds(arrival * 2 * pad + d * pad + k, 1)
                turned_z[d, k * rows:(k + 1) * rows] = (
                    value * cosine[near, :] + pltpu.roll(value, HALF, 1) * sine[near, :]
                )
        for d in range(2):
            for base in range(0, rows, together):
                mine = [turned_z[d, pl.ds(base + j, pad, stride=rows), :] for j in range(together)]
                for c in range(2):
                    for i in range(group):
                        start = c * HALF + i * sites
                        value = None
                        for j in range(together):
                            moved = pltpu.roll(mine[j], (j * SEAT - start) % LANES, 1)
                            value = moved if value is None else jnp.where(seat_of == j, moved, value)
                        low = ((c * group + i) * 2 + d) * pad
                        gathered[low:low + pad, base * SEAT:(base + together) * SEAT] = value.astype(jnp.bfloat16)
        origins = [origin_of(d, arrival) for d in range(2)]
        table = jnp.concatenate(
            [
                inverse[origins[d], at * pad:(at + 1) * pad]
                for at, d in ((2 * ci + d, d) for ci in range(2 * group) for d in range(2))
            ], axis=0
        )
        return lax.dot_general(
            gathered[...], table, (((0,), (0,)), ((), ())), preferred_element_type=jnp.float32
        )

    def finished(low, high):
        def one(arrival, carry):
            total[...] += finish(arrival)
            return carry

        lax.fori_loop(low, high, one, 0)

    for load in loads[3:5]:
        load.wait()
    turns = 3 * halves - (1 if halves > 1 else 0)
    shares = [0] + [rows // 8 + (rows - rows // 8) * turn // turns for turn in range(turns + 1)]
    transforms(shares[0], shares[1])
    for step in range(3):
        for h in range(halves):
            for d in range(2):
                receive(step, (d, h))
            at = halves * step + h + 1
            if at + 1 < len(shares):
                transforms(shares[at], shares[at + 1])
    loads[5].wait()

    def contracts(low, high, piece):
        lax.fori_loop(low, high, lambda arrival, carry: (contract(arrival, piece), carry)[1], 0)

    def both(step, carry):
        low = 2 * (step - 3)
        for h in range(halves):
            for d in range(2):
                receive(step, (d, h))
            for d in range(2):
                contracts(low, low + 2, (d, h))
            for arrival in (low, low + 1):
                for d in range(2):
                    send_z(arrival, (d, h))
            if h == 0:
                finished(jnp.maximum(low - 2, 0), low)
        return carry

    lax.fori_loop(3, 6, both, 0)

    def single(step, carry):
        for h in range(halves):
            for d in range(2):
                receive(step, (d, h))
            for d in range(2):
                contract(step, (d, h))
                send_z(step, (d, h))
            if h == 0:
                finished(step - 2, step - 1)
        return carry

    if n > 8:
        lax.fori_loop(6, n - 2, single, 0)
    for piece in pieces:
        contracts(n - 2, n - 1, piece)
        send_z(n - 2, piece)
    finished(n - 4, n - 2)
    for h in range(halves):
        for d in range(2):
            receive(n - 2, (d, h), True)
            contract(n - 1, (d, h))
            send_z(n - 1, (d, h))
        if h == 0:
            finished(n - 2, n - 1)
    spread_send[...] = spread[...]
    spread_copies = [
        pltpu.make_async_remote_copy(
            src_ref=spread_send, dst_ref=spread_recv.at[p - 1],
            send_sem=s_send_sem.at[p - 1], recv_sem=s_recv_sem.at[p - 1],
            device_id={"sens": lax.rem(me_s + p, sens_size)}, device_id_type=MESH,
        )
        for p in range(1, sens_size)
    ]
    for copy in spread_copies:
        copy.start()
    for step in range(n - 1):
        for piece in pieces:
            ring_copy(step, piece, False).wait_send()
    for arrival in range(n - 1):
        for piece in pieces:
            for copy in z_copies(arrival, piece):
                copy.wait_send()
    result = total[...] + finish(n - 1)
    for r in range(rows):
        out[r] = result[r * SEAT:r * SEAT + sites].astype(jnp.bfloat16)
    for copy in spread_copies:
        copy.wait()
    summed = spread[...]
    for p in range(1, sens_size):
        summed += spread_recv[p - 1]
    summed = jnp.broadcast_to(jnp.sum(summed, axis=0, keepdims=True), summed.shape)
    summed = summed + pltpu.roll(summed, HALF, 1)
    folded = summed
    for i in range(1, group):
        folded += pltpu.roll(summed, LANES - i * sites, 1)
    spread_out[...] = folded
    for piece in pieces:
        for copy in z_copies(n - 1, piece):
            copy.wait_send()


def on_device(freq_size, sens_size, samples, response_tiles, slot_sensor, sensor_noise, advance_offset):
    bins_dev, _, slots, sites = response_tiles.shape
    rows, _, step_count = samples.shape
    peers = sens_size - 1
    plan = Plan(bins_dev, slots, sites, 2 if peers * freq_size * 4 <= 1024 else 1)
    group, chunks, m, pad = plan.group, plan.chunks, plan.m, plan.pad
    forward, inverse = make_tables(freq_size, plan, step_count)
    tiles = response_tiles.transpose(0, 3, 1, 2)
    lane_tiles = -(-slots // LANES)
    count = len(plan.pieces)
    wide = -(-step_count // LANES) * LANES
    vmem = pl.BlockSpec(memory_space=pltpu.VMEM)
    anywhere = pl.BlockSpec(memory_space=pl.ANY)
    outlook, spread = pl.pallas_call(
        functools.partial(kernel, freq_size, sens_size, plan),
        out_shape=(
            jax.ShapeDtypeStruct((rows, sites, step_count), jnp.bfloat16),
            jax.ShapeDtypeStruct((8, LANES), jnp.float32),
        ),
        in_specs=[anywhere] * 7,
        out_specs=(vmem, vmem),
        scratch_shapes=[
            pltpu.VMEM(tiles.shape, jnp.bfloat16),
            pltpu.VMEM(samples.shape, jnp.bfloat16),
            pltpu.VMEM(forward.shape, jnp.bfloat16),
            pltpu.VMEM(inverse.shape, jnp.bfloat16),
            pltpu.SMEM(slot_sensor.shape, jnp.int32),
            pltpu.SMEM(sensor_noise.shape, jnp.float32),
            pltpu.SMEM(advance_offset.shape, jnp.int32),
            pltpu.SemaphoreType.DMA((6,)),
            pltpu.SemaphoreType.DMA((count,)),
            pltpu.VMEM((2, slots, LANES), jnp.float32),
            pltpu.VMEM((slots, wide), jnp.bfloat16),
            pltpu.VMEM((freq_size * 2 * pad, LANES), jnp.float32),
            pltpu.VMEM((freq_size * 2 * pad, LANES), jnp.float32),
            pltpu.VMEM((freq_size * 2 * pad, LANES), jnp.float32),
            pltpu.VMEM((2, freq_size, plan.held_rows, LANES), jnp.bfloat16),
            pltpu.VMEM((lane_tiles, freq_size * chunks * group * 2 * rows, LANES), jnp.float32),
            pltpu.VMEM((freq_size * 2 * m * rows, LANES), jnp.float32),
            pltpu.VMEM((freq_size * 2 * m, rows, LANES), jnp.bfloat16),
            pltpu.VMEM((peers, freq_size * 2 * m, rows, LANES), jnp.bfloat16),
            pltpu.VMEM((2, pad * rows, LANES), jnp.float32),
            pltpu.VMEM((4 * group * pad, rows * SEAT), jnp.bfloat16),
            pltpu.VMEM((rows * SEAT, step_count), jnp.float32),
            pltpu.VMEM((8, LANES), jnp.float32),
            pltpu.VMEM((8, LANES), jnp.float32),
            pltpu.VMEM((peers, 8, LANES), jnp.float32),
            pltpu.SemaphoreType.DMA((count, freq_size - 1)),
            pltpu.SemaphoreType.DMA((count, freq_size - 1)),
            pltpu.SemaphoreType.DMA((peers, freq_size * count)),
            pltpu.SemaphoreType.DMA((peers, freq_size * count)),
            pltpu.SemaphoreType.DMA((peers,)),
            pltpu.SemaphoreType.DMA((peers,)),
        ],
        compiler_params=pltpu.CompilerParams(
            collective_id=0, has_side_effects=True, vmem_limit_bytes=60 * 1024 * 1024
        ),
    )(
        tiles, samples, jnp.asarray(forward, jnp.bfloat16), jnp.asarray(inverse, jnp.bfloat16),
        slot_sensor, sensor_noise, advance_offset,
    )
    noise_spread = spread[0, :sites]
    return (outlook, noise_spread)


def solution(mesh):
    placed = (P("freq", "sens", None), P("freq", None, "sens", None), P("sens"), P(), P())
    return jax.shard_map(
        functools.partial(on_device, mesh.shape["freq"], mesh.shape["sens"]),
        mesh=mesh,
        in_specs=placed,
        out_specs=(P("freq", None, None), P()),
        check_vma=False,
    )
```

time: 89.8 us -> 75.8 us (0.84)
  local copies, waits for them, and re-layouts: 10.3 us -> 3.02 us
  Pallas kernels: 77.9 us -> 72 us
    pallas_call x1, Pallas kernels: 77.9 us -> 72 us  [on_device(): pl.pallas_call(functools.partial(kernel, freq_size, sens_size, plan), out...]
    reshape x1 -> x0, local copies, waits for them, and re-layouts: 3.84 us -> none  [on_device(): response_tiles.transpose(0, 3, 1, 2).reshape(bins_dev * 2 * sites, slots)]
    broadcast_in_dim x2 -> x0, local copies, waits for them, and re-layouts: 2.69 us -> none  [the longest x1 1.42 us: on_device(): slot_sensor[:, None]]
where the time goes in v1:
time: 75.8 us; the launch traced here: 75.7 us
  Pallas kernels  72 us (95%)
  local copies, waits for them, and re-layouts  3.02 us (4%)
    pallas_call x1, Pallas kernels, on_device(): pl.pallas_call(functools.partial(kernel, freq_size, sens_size, plan), out...  72 us
    unnamed x1, local copies, waits for them, and re-layouts  1.84 us

profile of v1, /device:TPU:0, one launch (start us, length us, event | category | flops | bytes accessed | tf_op | source)
XLA Modules:
  0.0 75.7 jit_solution(16439441458576415365)
XLA Ops:
  0.6 72.0 %shard_map.86 = (bf16[16,21,420]{2,1,0:T(8,128)(2,1)}, f32[8,128]{1,0:T(8,128)}) custom-call(bf16[56,21,2,152]{3,2,1,0:T(2,128)(2,1)} %bitcast.3, bf16[16,152,420]{2,1,0:T(8,128)(2,1)} %samples_in.1, bf16[2,456,420]{2,1,0:T(8,128)(2,1)} %constant.4.clone.forward_in, bf16[8,192,420]{2,1,0:T(8,128)(2,1)} %constant.5.clone.inverse_in, s32[152]{0:T(256)} %slots_in.1, ...), custom_call_target="tpu_custom_call" | custom-call | tf_op jit(solution)/shard_map/pallas_call | solution.py:453
  72.6 1.8 %copy.9 = bf16[16,21,420]{2,0,1:T(8,128)(2,1)} copy(bf16[16,21,420]{2,1,0:T(8,128)(2,1)} %get-tuple-element.6) | data formatting | bytes 564480
  74.5 1.2 %slice_bitcast_fusion = f32[21]{0:T(128)} fusion(f32[8,128]{1,0:T(8,128)} %get-tuple-element.5), kind=kLoop, calls=%fused_computation | loop fusion | bytes 168 | tf_op jit(solution)/shard_map/squeeze | solution.py:501

commit v2 on v1

--- a/solution.py
+++ b/solution.py
@@ -69,7 +69,7 @@
     out, spread_out,
     raw, samples, forward, inverse, ids, noise, offsets, load_sem, tile_sem,
     facts, live, cosine, sine, weight,
-    held, spectra, z_own, z_send, z_recv, turned_z, gathered, total, spread, spread_send, spread_recv,
+    held, spectra, z_own, z_send, z_recv, turned_z, gathered, total, staged, spread, spread_send, spread_recv,
     ring_send, ring_recv, z_send_sem, z_recv_sem, s_send_sem, s_recv_sem,
 ):
     rows, slots, step_count = samples.shape
@@ -345,61 +345,51 @@
 
     for load in loads[3:5]:
         load.wait()
-    turns = 3 * halves - (1 if halves > 1 else 0)
-    shares = [0] + [rows // 8 + (rows - rows // 8) * turn // turns for turn in range(turns + 1)]
-    transforms(shares[0], shares[1])
-    for step in range(3):
+    turns = 2 * halves - 1
+    early = rows * 5 // 16
+    shares = [early + (rows - early) * turn // turns for turn in range(turns + 1)]
+    transforms(0, early)
+
+    def contracts(low, high, piece):
+        lax.fori_loop(low, high, lambda arrival, carry: (contract(arrival, piece), carry)[1], 0)
+
+    for step in range(2):
         for h in range(halves):
             for d in range(2):
                 receive(step, (d, h))
-            at = halves * step + h + 1
-            if at + 1 < len(shares):
+            at = halves * step + h
+            if at < turns:
                 transforms(shares[at], shares[at + 1])
     loads[5].wait()
-
-    def contracts(low, high, piece):
-        lax.fori_loop(low, high, lambda arrival, carry: (contract(arrival, piece), carry)[1], 0)
-
-    def both(step, carry):
-        low = 2 * (step - 3)
+    for piece in pieces:
+        contracts(0, 2, piece)
+        for arrival in range(2):
+            send_z(arrival, piece)
+
+    def middle(step, carry):
         for h in range(halves):
             for d in range(2):
                 receive(step, (d, h))
-            for d in range(2):
-                contracts(low, low + 2, (d, h))
-            for arrival in (low, low + 1):
-                for d in range(2):
-                    send_z(arrival, (d, h))
             if h == 0:
-                finished(jnp.maximum(low - 2, 0), low)
-        return carry
-
-    lax.fori_loop(3, 6, both, 0)
-
-    def single(step, carry):
-        for h in range(halves):
-            for d in range(2):
-                receive(step, (d, h))
-            for d in range(2):
-                contract(step, (d, h))
-                send_z(step, (d, h))
-            if h == 0:
+                for piece in pieces:
+                    contract(step, piece)
+                    send_z(step, piece)
+            if h == halves - 1:
                 finished(step - 2, step - 1)
         return carry
 
-    if n > 8:
-        lax.fori_loop(6, n - 2, single, 0)
+    lax.fori_loop(2, n - 2, middle, 0)
     for piece in pieces:
-        contracts(n - 2, n - 1, piece)
+        contract(n - 2, piece)
         send_z(n - 2, piece)
-    finished(n - 4, n - 2)
+    finished(n - 4, n - 3)
     for h in range(halves):
         for d in range(2):
             receive(n - 2, (d, h), True)
             contract(n - 1, (d, h))
             send_z(n - 1, (d, h))
         if h == 0:
-            finished(n - 2, n - 1)
+            finished(n - 3, n - 2)
     spread_send[...] = spread[...]
     spread_copies = [
         pltpu.make_async_remote_copy(
@@ -418,9 +408,14 @@
         for piece in pieces:
             for copy in z_copies(arrival, piece):
                 copy.wait_send()
+    finished(n - 2, n - 1)
     result = total[...] + finish(n - 1)
-    for r in range(rows):
-        out[r] = result[r * SEAT:r * SEAT + sites].astype(jnp.bfloat16)
+    for tile in range(staged.shape[0]):
+        low, high = tile * LANES, min((tile + 1) * LANES, step_count)
+        for r in range(rows):
+            staged[tile, pl.ds(r, sites, stride=rows), :high - low] = result[r * SEAT:r * SEAT + sites, low:high]
+        for q in range(sites):
+            out[q, :, low:high] = staged[tile, q * rows:(q + 1) * rows, :high - low].astype(jnp.bfloat16)
     for copy in spread_copies:
         copy.wait()
     summed = spread[...]
@@ -450,10 +445,14 @@
     wide = -(-step_count // LANES) * LANES
     vmem = pl.BlockSpec(memory_space=pltpu.VMEM)
     anywhere = pl.BlockSpec(memory_space=pl.ANY)
+    operands = (
+        tiles, samples, jnp.asarray(forward, jnp.bfloat16), jnp.asarray(inverse, jnp.bfloat16),
+        slot_sensor, sensor_noise, advance_offset,
+    )
     outlook, spread = pl.pallas_call(
         functools.partial(kernel, freq_size, sens_size, plan),
         out_shape=(
-            jax.ShapeDtypeStruct((rows, sites, step_count), jnp.bfloat16),
+            jax.ShapeDtypeStruct((sites, rows, step_count), jnp.bfloat16),
             jax.ShapeDtypeStruct((8, LANES), jnp.float32),
         ),
         in_specs=[anywhere] * 7,
@@ -481,6 +480,7 @@
             pltpu.VMEM((2, pad * rows, LANES), jnp.float32),
             pltpu.VMEM((4 * group * pad, rows * SEAT), jnp.bfloat16),
             pltpu.VMEM((rows * SEAT, step_count), jnp.float32),
+            pltpu.VMEM((wide // LANES, sites * rows, LANES), jnp.float32),
             pltpu.VMEM((8, LANES), jnp.float32),
             pltpu.VMEM((8, LANES), jnp.float32),
             pltpu.VMEM((peers, 8, LANES), jnp.float32),
@@ -492,14 +492,11 @@
             pltpu.SemaphoreType.DMA((peers,)),
         ],
         compiler_params=pltpu.CompilerParams(
-            collective_id=0, has_side_effects=True, vmem_limit_bytes=60 * 1024 * 1024
+            collective_id=0, has_side_effects=True, vmem_limit_bytes=50 * 1024 * 1024
         ),
-    )(
-        tiles, samples, jnp.asarray(forward, jnp.bfloat16), jnp.asarray(inverse, jnp.bfloat16),
-        slot_sensor, sensor_noise, advance_offset,
-    )
+    )(*(pltpu.with_memory_space_constraint(array, pltpu.HBM) for array in operands))
     noise_spread = spread[0, :sites]
-    return (outlook, noise_spread)
+    return (outlook.transpose(1, 0, 2), noise_spread)
 
 
 def solution(mesh):

time: 75.8 us -> 70.3 us (0.927)
  Pallas kernels: 72 us -> 68.2 us
  local copies, waits for them, and re-layouts: 3.02 us -> 1.24 us
    pallas_call x1, Pallas kernels: 72 us -> 68.2 us  [on_device(): pl.pallas_call(functools.partial(kernel, freq_size, sens_size, plan), out...]
    unnamed x1, local copies, waits for them, and re-layouts: 1.84 us -> 0.73 us
where the time goes in v2:
time: 70.3 us; the launch traced here: 70.1 us
  Pallas kernels  68.2 us (97%)
  local copies, waits for them, and re-layouts  1.24 us (2%)
    pallas_call x1, Pallas kernels, on_device(): pl.pallas_call(functools.partial(kernel, freq_size, sens_size, plan), out...  68.2 us

profile of v2, /device:TPU:0, one launch (start us, length us, event | category | flops | bytes accessed | tf_op | source)
XLA Modules:
  0.0 70.1 jit_solution(5578701430522632936)
XLA Ops:
  0.6 68.2 %shard_map.86 = (bf16[21,16,420]{2,1,0:T(8,128)(2,1)S(1)}, f32[8,128]{1,0:T(8,128)S(1)}) custom-call(bf16[56,21,2,152]{3,2,1,0:T(2,128)(2,1)} %bitcast.5, bf16[16,152,420]{2,1,0:T(8,128)(2,1)} %samples_in.1, bf16[2,456,420]{2,1,0:T(8,128)(2,1)} %constant.4.clone.forward_in, bf16[8,192,420]{2,1,0:T(8,128)(2,1)} %constant.5.clone.inverse_in, s32[152]{0:T(256)} %slots_in.1, ...), custom_call_target="tpu_custom_call" | custom-call | tf_op jit(solution)/shard_map/pallas_call | solution.py:452
  68.9 0.5 slice_bitcast_fusion
  69.4 0.7 %copy.10 = bf16[16,21,420]{2,0,1:T(8,128)(2,1)} copy(bf16[16,21,420]{2,0,1:T(8,128)(2,1)S(1)} %bitcast.4) | data formatting | bytes 564480

commit v3 on v2

--- a/solution.py
+++ b/solution.py
@@ -136,7 +136,7 @@
         at = 2 * h + d
         return pltpu.make_async_remote_copy(
             src_ref=block, dst_ref=block,
-            send_sem=ring_send.at[at, step], recv_sem=ring_recv.at[at, step],
+            send_sem=ring_send.at[d], recv_sem=ring_recv.at[at, step],
             device_id={"freq": left if d else right}, device_id_type=MESH,
         )
 
@@ -277,11 +277,10 @@
         d, h = piece
         low, high = plan.spans[h]
         part = pl.ds(z_row(arrival, d, low), high - low)
-        at = arrival * len(pieces) + 2 * h + d
         return [
             pltpu.make_async_remote_copy(
                 src_ref=z_send.at[part], dst_ref=z_recv.at[p - 1, part],
-                send_sem=z_send_sem.at[p - 1, at], recv_sem=z_recv_sem.at[p - 1, at],
+                send_sem=z_send_sem.at[0], recv_sem=z_recv_sem.at[arrival],
                 device_id={"sens": lax.rem(me_s + p, sens_size)}, device_id_type=MESH,
             )
             for p in range(1, sens_size)
@@ -300,9 +299,8 @@
     seat_of = lax.broadcasted_iota(jnp.int32, (pad, LANES), 1) // SEAT
 
     def finish(arrival):
-        for piece in pieces:
-            for copy in z_copies(arrival, piece):
-                copy.wait_recv()
+        landed = z_recv.at[:, pl.ds(z_row(arrival, 0, 0), 2 * m)]
+        pltpu.make_async_copy(landed, landed, z_recv_sem.at[arrival]).wait()
         for d in range(2):
             for k in range(m):
                 at = z_row(arrival, d, k)
@@ -394,20 +392,16 @@
     spread_copies = [
         pltpu.make_async_remote_copy(
             src_ref=spread_send, dst_ref=spread_recv.at[p - 1],
-            send_sem=s_send_sem.at[p - 1], recv_sem=s_recv_sem.at[p - 1],
+            send_sem=s_send_sem.at[0], recv_sem=s_recv_sem.at[0],
             device_id={"sens": lax.rem(me_s + p, sens_size)}, device_id_type=MESH,
         )
         for p in range(1, sens_size)
     ]
     for copy in spread_copies:
         copy.start()
-    for step in range(n - 1):
-        for piece in pieces:
-            ring_copy(step, piece, False).wait_send()
-    for arrival in range(n - 1):
-        for piece in pieces:
-            for copy in z_copies(arrival, piece):
-                copy.wait_send()
+    for d in range(2):
+        gone = held.at[d, pl.ds(0, n - 1), pl.ds(0, plan.rows[d])]
+        pltpu.make_async_copy(gone, gone, ring_send.at[d]).wait()
     finished(n - 2, n - 1)
     result = total[...] + finish(n - 1)
     for tile in range(staged.shape[0]):
@@ -416,8 +410,8 @@
             staged[tile, pl.ds(r, sites, stride=rows), :high - low] = result[r * SEAT:r * SEAT + sites, low:high]
         for q in range(sites):
             out[q, :, low:high] = staged[tile, q * rows:(q + 1) * rows, :high - low].astype(jnp.bfloat16)
-    for copy in spread_copies:
-        copy.wait()
+    pltpu.make_async_copy(spread_recv, spread_recv, s_send_sem.at[0]).wait()
+    pltpu.make_async_copy(spread_recv, spread_recv, s_recv_sem.at[0]).wait()
     summed = spread[...]
     for p in range(1, sens_size):
         summed += spread_recv[p - 1]
@@ -427,16 +421,14 @@
     for i in range(1, group):
         folded += pltpu.roll(summed, LANES - i * sites, 1)
     spread_out[...] = folded
-    for piece in pieces:
-        for copy in z_copies(n - 1, piece):
-            copy.wait_send()
+    pltpu.make_async_copy(z_recv, z_recv, z_send_sem.at[0]).wait()
 
 
 def on_device(freq_size, sens_size, samples, response_tiles, slot_sensor, sensor_noise, advance_offset):
     bins_dev, _, slots, sites = response_tiles.shape
     rows, _, step_count = samples.shape
     peers = sens_size - 1
-    plan = Plan(bins_dev, slots, sites, 2 if peers * freq_size * 4 <= 1024 else 1)
+    plan = Plan(bins_dev, slots, sites, 2)
     group, chunks, m, pad = plan.group, plan.chunks, plan.m, plan.pad
     forward, inverse = make_tables(freq_size, plan, step_count)
     tiles = response_tiles.transpose(0, 3, 1, 2)
@@ -484,12 +476,12 @@
             pltpu.VMEM((8, LANES), jnp.float32),
             pltpu.VMEM((8, LANES), jnp.float32),
             pltpu.VMEM((peers, 8, LANES), jnp.float32),
+            pltpu.SemaphoreType.DMA((2,)),
             pltpu.SemaphoreType.DMA((count, freq_size - 1)),
-            pltpu.SemaphoreType.DMA((count, freq_size - 1)),
-            pltpu.SemaphoreType.DMA((peers, freq_size * count)),
-            pltpu.SemaphoreType.DMA((peers, freq_size * count)),
-            pltpu.SemaphoreType.DMA((peers,)),
-            pltpu.SemaphoreType.DMA((peers,)),
+            pltpu.SemaphoreType.DMA((1,)),
+            pltpu.SemaphoreType.DMA((freq_size,)),
+            pltpu.SemaphoreType.DMA((1,)),
+            pltpu.SemaphoreType.DMA((1,)),
         ],
         compiler_params=pltpu.CompilerParams(
             collective_id=0, has_side_effects=True, vmem_limit_bytes=50 * 1024 * 1024

time: 70.3 us -> 68.3 us (0.972)
  Pallas kernels: 68.2 us -> 66.3 us
    pallas_call x1, Pallas kernels: 68.2 us -> 66.3 us  [on_device(): pl.pallas_call(functools.partial(kernel, freq_size, sens_size, plan), out...]
where the time goes in v3:
time: 68.3 us; the launch traced here: 68.2 us
  Pallas kernels  66.3 us (97%)
  local copies, waits for them, and re-layouts  1.24 us (2%)
    pallas_call x1, Pallas kernels, on_device(): pl.pallas_call(functools.partial(kernel, freq_size, sens_size, plan), out...  66.3 us

profile of v3, /device:TPU:0, one launch (start us, length us, event | category | flops | bytes accessed | tf_op | source)
XLA Modules:
  0.0 68.2 jit_solution(5719460335898894402)
XLA Ops:
  0.6 66.3 %shard_map.86 = (bf16[21,16,420]{2,1,0:T(8,128)(2,1)S(1)}, f32[8,128]{1,0:T(8,128)S(1)}) custom-call(bf16[56,21,2,152]{3,2,1,0:T(2,128)(2,1)} %bitcast.5, bf16[16,152,420]{2,1,0:T(8,128)(2,1)} %samples_in.1, bf16[2,456,420]{2,1,0:T(8,128)(2,1)} %constant.4.clone.forward_in, bf16[8,192,420]{2,1,0:T(8,128)(2,1)} %constant.5.clone.inverse_in, s32[152]{0:T(256)} %slots_in.1, ...), custom_call_target="tpu_custom_call" | custom-call | tf_op jit(solution)/shard_map/pallas_call | solution.py:444
  66.9 0.5 slice_bitcast_fusion
  67.5 0.7 %copy.10 = bf16[16,21,420]{2,0,1:T(8,128)(2,1)} copy(bf16[16,21,420]{2,0,1:T(8,128)(2,1)S(1)} %bitcast.4) | data formatting | bytes 564480

commit v4 on v3

--- a/solution.py
+++ b/solution.py
@@ -16,12 +16,16 @@
 
 
 class Plan:
-    def __init__(self, bins_dev, slots, sites, halves):
+    def __init__(self, bins_dev, slots, sites):
         self.bins_dev, self.slots, self.sites = bins_dev, slots, sites
         self.group = HALF // sites
         self.chunks = -(-bins_dev // self.group)
         full = self.chunks // 2
-        cut = -(-slots // 32) * 16
+        last = self.chunks - 1
+        loose = self.group == 3 and bins_dev - last * 3 == 2 and last > 0
+        self.moved = slots // 24 * 8 if loose else 0
+        self.kept = slots - self.moved
+        cut = (self.kept + 16) // 32 * 16
         plus = [(c, 0, slots) for c in range(full)]
         minus = [(c, 0, slots) for c in range(self.chunks - full, self.chunks)]
         if self.chunks % 2:
@@ -30,18 +34,25 @@
         self.parts = (plus, minus)
         self.m = len(plus)
         self.pad = -(-self.m // 16) * 16
-        self.rows = [sum(hi - lo for _, lo, hi in part) for part in self.parts]
+        self.rows = [sum(map(self.height, part)) for part in self.parts]
         self.held_rows = -(-max(self.rows) // 16) * 16
-        ends = [-(-self.m * h // halves) for h in range(halves + 1)]
-        self.halves = halves
+        ends = sorted({0, -(-self.m * 3 // 10), -(-self.m * 7 // 10), self.m})
+        self.halves = halves = len(ends) - 1
         self.spans = list(zip(ends[:-1], ends[1:]))
         self.pieces = [(d, h) for h in range(halves) for d in range(2)]
 
     def size(self, chunk):
         return min(self.group, self.bins_dev - chunk * self.group)
 
+    def packed(self, chunk):
+        return self.moved > 0 and chunk == self.chunks - 1
+
+    def height(self, entry):
+        chunk, low, high = entry
+        return self.kept if self.packed(chunk) else high - low
+
     def row(self, d, k):
-        return sum(hi - lo for _, lo, hi in self.parts[d][:k])
+        return sum(map(self.height, self.parts[d][:k]))
 
 
 def make_tables(freq_size, plan, step_count):
@@ -68,13 +79,13 @@
     tiles_in, samples_in, forward_in, inverse_in, slots_in, noise_in, offsets_in,
     out, spread_out,
     raw, samples, forward, inverse, ids, noise, offsets, load_sem, tile_sem,
-    facts, live, cosine, sine, weight,
+    facts, facts_packed, live, cosine, sine, weight,
     held, spectra, z_own, z_send, z_recv, turned_z, gathered, total, staged, spread, spread_send, spread_recv,
     ring_send, ring_recv, z_send_sem, z_recv_sem, s_send_sem, s_recv_sem,
 ):
     rows, slots, step_count = samples.shape
     n, group, chunks, sites, m, pad = freq_size, plan.group, plan.chunks, plan.sites, plan.m, plan.pad
-    bins_dev = plan.bins_dev
+    bins_dev, kept, moved = plan.bins_dev, plan.kept, plan.moved
     per_bin = 2 * rows
     lane_tiles = spectra.shape[0]
     period = 2 * n * bins_dev
@@ -157,6 +168,18 @@
                 preferred_element_type=jnp.float32,
             ).astype(jnp.bfloat16)
             at = plan.row(d, k)
+            if plan.packed(chunk):
+                aside = []
+                for i in range(size):
+                    one = raw[chunk * group + i].reshape(sites * 2, slots)
+                    aside.append(lax.dot_general(
+                        one, sorter[size * sites * 2:], (((0,), (0,)), ((), ())),
+                        preferred_element_type=jnp.float32,
+                    )[kept:])
+                aside.append(jnp.zeros((kept - size * moved, LANES), jnp.float32))
+                both = turned[:kept].astype(jnp.float32) + jnp.concatenate(aside, axis=0)
+                held[d, me_f, at:at + kept] = both.astype(jnp.bfloat16)
+                continue
             held[d, me_f, at:at + high - low] = turned[low:high]
             if not whole:
                 at = plan.row(1, m - 1)
@@ -181,6 +204,10 @@
         return carry
 
     lax.fori_loop(0, slots, fact, 0, unroll=8)
+    if moved:
+        aside = [facts[0, kept:]] * (group - 1) + [jnp.zeros((kept - (group - 1) * moved, LANES), jnp.float32)]
+        spare = lax.broadcasted_iota(jnp.int32, (kept, LANES), 1) % HALF // sites == group - 1
+        facts_packed[...] = jnp.where(spare, jnp.concatenate(aside, axis=0), facts[0, :kept])
     there = facts[1].astype(jnp.bfloat16)
     live[...] = jnp.concatenate([there] * (live.shape[1] // LANES), axis=1)
     spread[...] = jnp.zeros_like(spread)
@@ -205,6 +232,10 @@
     within = chunk_of * group + inside // sites
     alive = (within < bins_dev) & (inside < group * sites) & (seat % pad < m)
     turning = 2.0 * math.pi / period
+    seats = [d * pad + k for d in range(2) for k in range(m) if plan.packed(plan.parts[d][k][0])]
+    extra = jnp.zeros((2 * pad, LANES), jnp.float32)
+    for row in seats:
+        extra = jnp.where((seat == row) & (inside // sites == group - 1), 2.0 / period, extra)
 
     def phase(arrival, carry):
         block = jnp.where(side == 0, origin_of(0, arrival), origin_of(1, arrival))
@@ -214,7 +245,7 @@
         here = pl.ds(pl.multiple_of(arrival * 2 * pad, 2 * pad), 2 * pad)
         cosine[here, :] = jnp.cos(angle)
         sine[here, :] = jnp.sin(angle) * jnp.where(place < HALF, -1.0, 1.0)
-        weight[here, :] = jnp.where(alive, jnp.where(bins == 0, 1.0, 2.0) / period, 0.0)
+        weight[here, :] = jnp.where(alive, jnp.where(bins == 0, 1.0, 2.0) / period, 0.0) + extra
         return carry
 
     lax.fori_loop(0, n, phase, 0)
@@ -240,6 +271,20 @@
     def z_row(arrival, d, k):
         return (arrival * 2 + d) * m + k
 
+    def aside_of(parts):
+        spot = lax.broadcasted_iota(jnp.int32, (per_bin, LANES), 1)
+        lines = []
+        for i in range(group - 1):
+            line = jnp.zeros((per_bin, LANES), jnp.float32)
+            for tile, part in enumerate(parts):
+                low, high = max(kept, tile * LANES), min(slots, (tile + 1) * LANES)
+                if low < high:
+                    turned = pltpu.roll(part[i * per_bin:(i + 1) * per_bin], (i * moved - kept + tile * LANES) % LANES, 1)
+                    at = i * moved - kept
+                    line = jnp.where((spot >= at + low) & (spot < at + high), turned, line)
+            lines.append(line)
+        return jnp.concatenate(lines, axis=0)[:, :kept].astype(jnp.bfloat16)
+
     def contract(arrival, piece):
         d, h = piece
         origin = origin_of(d, arrival)
@@ -247,12 +292,15 @@
         for k in range(*plan.spans[h]):
             chunk, low, high = plan.parts[d][k]
             row = plan.row(d, k)
-            weights = held[d, origin, row:row + high - low]
+            height = plan.height(plan.parts[d][k])
+            weights = held[d, origin, row:row + height]
             first = pl.multiple_of((origin * chunks + chunk) * (group * per_bin), group * per_bin)
             parts = [spectra[tile, pl.ds(first, group * per_bin), :] for tile in range(lane_tiles)]
             spec = jnp.concatenate(parts, axis=1)[:, :slots].astype(jnp.bfloat16)
             filled = weights
-            if high - low < slots:
+            if plan.packed(chunk):
+                spec = spec[:, :kept]
+            elif high - low < slots:
                 filled = jnp.concatenate(
                     ([jnp.zeros((low, LANES), jnp.bfloat16)] if low else []) + [weights]
                     + ([jnp.zeros((slots - high, LANES), jnp.bfloat16)] if high < slots else []), axis=0
@@ -263,13 +311,20 @@
                 for c in range(2):
                     at = i * per_bin + c * rows
                     picked[c] = jnp.where(which == i, product[at:at + rows], picked[c])
+            if plan.packed(chunk):
+                beside = jnp.dot(aside_of(parts), weights, preferred_element_type=jnp.float32)
+                for i in range(group - 1):
+                    for c in range(2):
+                        at = i * per_bin + c * rows
+                        back = pltpu.roll(beside[at:at + rows], LANES - (group - 1 - i) * sites, 1)
+                        picked[c] += jnp.where(which == i, back, 0.0)
             value = picked[0] + sign * pltpu.roll(picked[1], HALF, 1)
             at = z_row(arrival, d, k)
             z_own[pl.ds(pl.multiple_of(at * rows, rows), rows), :] = value
             z_send[at] = value.astype(jnp.bfloat16)
             wide = weights.astype(jnp.float32)
-            power = wide * wide * facts[0, low:high]
-            power = power.reshape((high - low) // 8, 8, LANES).sum(axis=0)
+            known = facts_packed[...] if plan.packed(chunk) else facts[0, low:high]
+            power = (wide * wide * known).reshape(height // 8, 8, LANES).sum(axis=0)
             noisy += power * weight[pl.ds(arrival * 2 * pad + d * pad + k, 1), :]
         spread[...] = noisy
 
@@ -428,7 +483,7 @@
     bins_dev, _, slots, sites = response_tiles.shape
     rows, _, step_count = samples.shape
     peers = sens_size - 1
-    plan = Plan(bins_dev, slots, sites, 2)
+    plan = Plan(bins_dev, slots, sites)
     group, chunks, m, pad = plan.group, plan.chunks, plan.m, plan.pad
     forward, inverse = make_tables(freq_size, plan, step_count)
     tiles = response_tiles.transpose(0, 3, 1, 2)
@@ -460,6 +515,7 @@
             pltpu.SemaphoreType.DMA((6,)),
             pltpu.SemaphoreType.DMA((count,)),
             pltpu.VMEM((2, slots, LANES), jnp.float32),
+            pltpu.VMEM((plan.kept, LANES), jnp.float32),
             pltpu.VMEM((slots, wide), jnp.bfloat16),
             pltpu.VMEM((freq_size * 2 * pad, LANES), jnp.float32),
             pltpu.VMEM((freq_size * 2 * pad, LANES), jnp.float32),

time: 68.3 us -> 67.4 us (0.987)
  Pallas kernels: 66.3 us -> 65.4 us
    pallas_call x1, Pallas kernels: 66.3 us -> 65.4 us  [on_device(): pl.pallas_call(functools.partial(kernel, freq_size, sens_size, plan), out...]
where the time goes in v4:
time: 67.4 us; the launch traced here: 67.2 us
  Pallas kernels  65.4 us (97%)
  local copies, waits for them, and re-layouts  1.24 us (2%)
    pallas_call x1, Pallas kernels, on_device(): pl.pallas_call(functools.partial(kernel, freq_size, sens_size, plan), out...  65.4 us

profile of v4, /device:TPU:0, one launch (start us, length us, event | category | flops | bytes accessed | tf_op | source)
XLA Modules:
  0.0 67.2 jit_solution(16704770397392445286)
XLA Ops:
  0.6 65.4 %shard_map.86 = (bf16[21,16,420]{2,1,0:T(8,128)(2,1)S(1)}, f32[8,128]{1,0:T(8,128)S(1)}) custom-call(bf16[56,21,2,152]{3,2,1,0:T(2,128)(2,1)} %bitcast.5, bf16[16,152,420]{2,1,0:T(8,128)(2,1)} %samples_in.1, bf16[2,456,420]{2,1,0:T(8,128)(2,1)} %constant.4.clone.forward_in, bf16[8,192,420]{2,1,0:T(8,128)(2,1)} %constant.5.clone.inverse_in, s32[152]{0:T(256)} %slots_in.1, ...), custom_call_target="tpu_custom_call" | custom-call | tf_op jit(solution)/shard_map/pallas_call | solution.py:499
  66.0 0.5 slice_bitcast_fusion
  66.5 0.7 %copy.10 = bf16[16,21,420]{2,0,1:T(8,128)(2,1)} copy(bf16[16,21,420]{2,0,1:T(8,128)(2,1)S(1)} %bitcast.4) | data formatting | bytes 564480

commit v5 on v4

--- a/solution.py
+++ b/solution.py
@@ -23,7 +23,7 @@
         full = self.chunks // 2
         last = self.chunks - 1
         loose = self.group == 3 and bins_dev - last * 3 == 2 and last > 0
-        self.moved = slots // 24 * 8 if loose else 0
+        self.moved = slots // 24 * 8 if loose and slots - slots // 24 * 8 <= LANES else 0
         self.kept = slots - self.moved
         cut = (self.kept + 16) // 32 * 16
         plus = [(c, 0, slots) for c in range(full)]
@@ -36,7 +36,7 @@
         self.pad = -(-self.m // 16) * 16
         self.rows = [sum(map(self.height, part)) for part in self.parts]
         self.held_rows = -(-max(self.rows) // 16) * 16
-        ends = sorted({0, -(-self.m * 3 // 10), -(-self.m * 7 // 10), self.m})
+        ends = sorted({0, -(-self.m * 3 // 10), self.m - self.m // 5, self.m})
         self.halves = halves = len(ends) - 1
         self.spans = list(zip(ends[:-1], ends[1:]))
         self.pieces = [(d, h) for h in range(halves) for d in range(2)]
@@ -108,14 +108,6 @@
 
     def origin_of(d, arrival):
         return along(arrival if d else -arrival)
-
-    right, left = along(1), along(-1)
-    barrier = pltpu.get_barrier_semaphore()
-    for neighbour in (left, right):
-        pl.semaphore_signal(barrier, inc=1, device_id={"freq": neighbour}, device_id_type=MESH)
-    for d in range(1, sens_size):
-        peer = lax.rem(me_s + d, sens_size)
-        pl.semaphore_signal(barrier, inc=1, device_id={"sens": peer}, device_id_type=MESH)
 
     tile_loads = []
     for at, (d, h) in enumerate(pieces):
@@ -138,6 +130,14 @@
     ]
     for load in sum(tile_loads, []) + loads:
         load.start()
+
+    right, left = along(1), along(-1)
+    barrier = pltpu.get_barrier_semaphore()
+    for neighbour in (left, right):
+        pl.semaphore_signal(barrier, inc=1, device_id={"freq": neighbour}, device_id_type=MESH)
+    for d in range(1, sens_size):
+        peer = lax.rem(me_s + d, sens_size)
+        pl.semaphore_signal(barrier, inc=1, device_id={"sens": peer}, device_id_type=MESH)
 
     def ring_copy(step, piece, received):
         d, h = piece
@@ -321,28 +321,28 @@
             value = picked[0] + sign * pltpu.roll(picked[1], HALF, 1)
             at = z_row(arrival, d, k)
             z_own[pl.ds(pl.multiple_of(at * rows, rows), rows), :] = value
-            z_send[at] = value.astype(jnp.bfloat16)
+            z_send[arrival, d, k] = value.astype(jnp.bfloat16)
             wide = weights.astype(jnp.float32)
             known = facts_packed[...] if plan.packed(chunk) else facts[0, low:high]
             power = (wide * wide * known).reshape(height // 8, 8, LANES).sum(axis=0)
             noisy += power * weight[pl.ds(arrival * 2 * pad + d * pad + k, 1), :]
         spread[...] = noisy
 
-    def z_copies(arrival, piece):
+    def z_copies(arrival, piece, last):
         d, h = piece
         low, high = plan.spans[h]
-        part = pl.ds(z_row(arrival, d, low), high - low)
+        part = pl.ds(low, high - low)
         return [
             pltpu.make_async_remote_copy(
-                src_ref=z_send.at[part], dst_ref=z_recv.at[p - 1, part],
-                send_sem=z_send_sem.at[0], recv_sem=z_recv_sem.at[arrival],
+                src_ref=z_send.at[arrival, d, part], dst_ref=z_recv.at[p - 1, arrival, d, part],
+                send_sem=z_send_sem.at[0], recv_sem=z_recv_sem.at[n if last else arrival],
                 device_id={"sens": lax.rem(me_s + p, sens_size)}, device_id_type=MESH,
             )
             for p in range(1, sens_size)
         ]
 
-    def send_z(arrival, piece):
-        for copy in z_copies(arrival, piece):
+    def send_z(arrival, piece, last=False):
+        for copy in z_copies(arrival, piece, last):
             copy.start()
 
     def receive(step, piece, last=False):
@@ -353,45 +353,54 @@
     together = LANES // SEAT
     seat_of = lax.broadcasted_iota(jnp.int32, (pad, LANES), 1) // SEAT
 
-    def finish(arrival):
-        landed = z_recv.at[:, pl.ds(z_row(arrival, 0, 0), 2 * m)]
-        pltpu.make_async_copy(landed, landed, z_recv_sem.at[arrival]).wait()
+    def combine(arrival, low, high):
         for d in range(2):
-            for k in range(m):
+            for k in range(low, high):
                 at = z_row(arrival, d, k)
                 value = z_own[pl.ds(pl.multiple_of(at * rows, rows), rows), :]
                 for p in range(1, sens_size):
-                    value += z_recv[p - 1, at].astype(jnp.float32)
+                    value += z_recv[p - 1, arrival, d, k].astype(jnp.float32)
                 near = pl.ds(arrival * 2 * pad + d * pad + k, 1)
                 turned_z[d, k * rows:(k + 1) * rows] = (
                     value * cosine[near, :] + pltpu.roll(value, HALF, 1) * sine[near, :]
                 )
-        for d in range(2):
-            for base in range(0, rows, together):
-                mine = [turned_z[d, pl.ds(base + j, pad, stride=rows), :] for j in range(together)]
-                for c in range(2):
-                    for i in range(group):
-                        start = c * HALF + i * sites
-                        value = None
-                        for j in range(together):
-                            moved = pltpu.roll(mine[j], (j * SEAT - start) % LANES, 1)
-                            value = moved if value is None else jnp.where(seat_of == j, moved, value)
-                        low = ((c * group + i) * 2 + d) * pad
-                        gathered[low:low + pad, base * SEAT:(base + together) * SEAT] = value.astype(jnp.bfloat16)
+
+    def table_of(arrival):
         origins = [origin_of(d, arrival) for d in range(2)]
-        table = jnp.concatenate(
+        return jnp.concatenate(
             [
                 inverse[origins[d], at * pad:(at + 1) * pad]
                 for at, d in ((2 * ci + d, d) for ci in range(2 * group) for d in range(2))
             ], axis=0
         )
-        return lax.dot_general(
-            gathered[...], table, (((0,), (0,)), ((), ())), preferred_element_type=jnp.float32
-        )
+
+    def gather(base):
+        for d in range(2):
+            mine = [turned_z[d, pl.ds(base + j, pad, stride=rows), :] for j in range(together)]
+            for c in range(2):
+                for i in range(group):
+                    start = c * HALF + i * sites
+                    value = None
+                    for j in range(together):
+                        moved_to = pltpu.roll(mine[j], (j * SEAT - start) % LANES, 1)
+                        value = moved_to if value is None else jnp.where(seat_of == j, moved_to, value)
+                    low = ((c * group + i) * 2 + d) * pad
+                    gathered[low:low + pad, base * SEAT:(base + together) * SEAT] = value.astype(jnp.bfloat16)
+
+    def times(block, table):
+        return lax.dot_general(block, table, (((0,), (0,)), ((), ())), preferred_element_type=jnp.float32)
+
+    def invert(arrival):
+        for base in range(0, rows, together):
+            gather(base)
+        return times(gathered[...], table_of(arrival))
 
     def finished(low, high):
         def one(arrival, carry):
-            total[...] += finish(arrival)
+            landed = z_recv.at[:, arrival]
+            pltpu.make_async_copy(landed, landed, z_recv_sem.at[arrival]).wait()
+            combine(arrival, 0, m)
+            total[...] += invert(arrival)
             return carry
 
         lax.fori_loop(low, high, one, 0)
@@ -436,14 +445,6 @@
         contract(n - 2, piece)
         send_z(n - 2, piece)
     finished(n - 4, n - 3)
-    for h in range(halves):
-        for d in range(2):
-            receive(n - 2, (d, h), True)
-            contract(n - 1, (d, h))
-            send_z(n - 1, (d, h))
-        if h == 0:
-            finished(n - 3, n - 2)
-    spread_send[...] = spread[...]
     spread_copies = [
         pltpu.make_async_remote_copy(
             src_ref=spread_send, dst_ref=spread_recv.at[p - 1],
@@ -452,31 +453,65 @@
         )
         for p in range(1, sens_size)
     ]
-    for copy in spread_copies:
-        copy.start()
+    for h in range(halves):
+        for d in range(2):
+            receive(n - 2, (d, h), True)
+            contract(n - 1, (d, h))
+            if (d, h) == pieces[-1]:
+                spread_send[...] = spread[...]
+                for copy in spread_copies:
+                    copy.start()
+            send_z(n - 1, (d, h), h == halves - 1)
+        if h == 0:
+            finished(n - 3, n - 2)
     for d in range(2):
         gone = held.at[d, pl.ds(0, n - 1), pl.ds(0, plan.rows[d])]
         pltpu.make_async_copy(gone, gone, ring_send.at[d]).wait()
     finished(n - 2, n - 1)
-    result = total[...] + finish(n - 1)
+    split = plan.spans[-1][0]
+    for low, high, at in ((0, split, n - 1), (split, m, n)):
+        if at == n:
+            pltpu.make_async_copy(spread_recv, spread_recv, s_send_sem.at[0]).wait()
+            pltpu.make_async_copy(spread_recv, spread_recv, s_recv_sem.at[0]).wait()
+            summed = spread[...]
+            for p in range(1, sens_size):
+                summed += spread_recv[p - 1]
+            summed = jnp.broadcast_to(jnp.sum(summed, axis=0, keepdims=True), summed.shape)
+            summed = summed + pltpu.roll(summed, HALF, 1)
+            folded = summed
+            for i in range(1, group):
+                folded += pltpu.roll(summed, LANES - i * sites, 1)
+            spread_out[...] = folded[:1, :sites]
+        landed = z_recv.at[:, n - 1, :, pl.ds(low, high - low)]
+        pltpu.make_async_copy(landed, landed, z_recv_sem.at[at]).wait()
+        combine(n - 1, low, high)
+    table = table_of(n - 1)
+    for base in range(0, rows, together):
+        gather(base)
+        span = slice(base * SEAT, (base + together) * SEAT)
+        result = total[span] + times(gathered[:, span], table)
+        for tile in range(staged.shape[0]):
+            low, high = tile * LANES, min((tile + 1) * LANES, step_count)
+            for j in range(together):
+                staged[tile, pl.ds(base + j, sites, stride=rows), :high - low] = (
+                    result[j * SEAT:j * SEAT + sites, low:high]
+                )
     for tile in range(staged.shape[0]):
         low, high = tile * LANES, min((tile + 1) * LANES, step_count)
-        for r in range(rows):
-            staged[tile, pl.ds(r, sites, stride=rows), :high - low] = result[r * SEAT:r * SEAT + sites, low:high]
         for q in range(sites):
             out[q, :, low:high] = staged[tile, q * rows:(q + 1) * rows, :high - low].astype(jnp.bfloat16)
-    pltpu.make_async_copy(spread_recv, spread_recv, s_send_sem.at[0]).wait()
-    pltpu.make_async_copy(spread_recv, spread_recv, s_recv_sem.at[0]).wait()
-    summed = spread[...]
-    for p in range(1, sens_size):
-        summed += spread_recv[p - 1]
-    summed = jnp.broadcast_to(jnp.sum(summed, axis=0, keepdims=True), summed.shape)
-    summed = summed + pltpu.roll(summed, HALF, 1)
-    folded = summed
-    for i in range(1, group):
-        folded += pltpu.roll(summed, LANES - i * sites, 1)
-    spread_out[...] = folded
     pltpu.make_async_copy(z_recv, z_recv, z_send_sem.at[0]).wait()
+
+
+def hand_out(outlook_in, spread_in, outlook_out, spread_out, sem):
+    copies = [
+        pltpu.make_async_copy(source, target, sem.at[at])
+        for at, (source, target) in enumerate(((outlook_in, outlook_out), (spread_in, spread_out)))
+    ]
+    for copy in copies:
+        copy.start()
+    for copy in copies:
+        copy.wait()
 
 
 def on_device(freq_size, sens_size, samples, response_tiles, slot_sensor, sensor_noise, advance_offset):
@@ -500,7 +535,7 @@
         functools.partial(kernel, freq_size, sens_size, plan),
         out_shape=(
             jax.ShapeDtypeStruct((sites, rows, step_count), jnp.bfloat16),
-            jax.ShapeDtypeStruct((8, LANES), jnp.float32),
+            jax.ShapeDtypeStruct((1, sites), jnp.float32),
         ),
         in_specs=[anywhere] * 7,
         out_specs=(vmem, vmem),
@@ -523,8 +558,8 @@
             pltpu.VMEM((2, freq_size, plan.held_rows, LANES), jnp.bfloat16),
             pltpu.VMEM((lane_tiles, freq_size * chunks * group * 2 * rows, LANES), jnp.float32),
             pltpu.VMEM((freq_size * 2 * m * rows, LANES), jnp.float32),
-            pltpu.VMEM((freq_size * 2 * m, rows, LANES), jnp.bfloat16),
-            pltpu.VMEM((peers, freq_size * 2 * m, rows, LANES), jnp.bfloat16),
+            pltpu.VMEM((freq_size, 2, m, rows, LANES), jnp.bfloat16),
+            pltpu.VMEM((peers, freq_size, 2, m, rows, LANES), jnp.bfloat16),
             pltpu.VMEM((2, pad * rows, LANES), jnp.float32),
             pltpu.VMEM((4 * group * pad, rows * SEAT), jnp.bfloat16),
             pltpu.VMEM((rows * SEAT, step_count), jnp.float32),
@@ -535,7 +570,7 @@
             pltpu.SemaphoreType.DMA((2,)),
             pltpu.SemaphoreType.DMA((count, freq_size - 1)),
             pltpu.SemaphoreType.DMA((1,)),
-            pltpu.SemaphoreType.DMA((freq_size,)),
+            pltpu.SemaphoreType.DMA((freq_size + 1,)),
             pltpu.SemaphoreType.DMA((1,)),
             pltpu.SemaphoreType.DMA((1,)),
         ],
@@ -543,8 +578,18 @@
             collective_id=0, has_side_effects=True, vmem_limit_bytes=50 * 1024 * 1024
         ),
     )(*(pltpu.with_memory_space_constraint(array, pltpu.HBM) for array in operands))
-    noise_spread = spread[0, :sites]
-    return (outlook.transpose(1, 0, 2), noise_spread)
+    outlook, spread = pl.pallas_call(
+        hand_out,
+        out_shape=(
+            jax.ShapeDtypeStruct(outlook.shape, outlook.dtype),
+            jax.ShapeDtypeStruct(spread.shape, spread.dtype),
+        ),
+        in_specs=[anywhere] * 2,
+        out_specs=(anywhere, anywhere),
+        scratch_shapes=[pltpu.SemaphoreType.DMA((2,))],
+        compiler_params=pltpu.CompilerParams(vmem_limit_bytes=1024 * 1024),
+    )(outlook, spread)
+    return (outlook.transpose(1, 0, 2), spread.reshape(sites))
 
 
 def solution(mesh):

time: 67.4 us -> 66.7 us (0.990)
  local copies, waits for them, and re-layouts: 1.24 us -> 0 us
    pallas_call x0 -> x1, Pallas kernels: none -> 0.75 us  [on_device(): pl.pallas_call(hand_out, out_shape=(jax.ShapeDtypeStruct(outlook.shape, o...]
    unnamed x1 -> x0, local copies, waits for them, and re-layouts: 0.73 us -> none
where the time goes in v5:
time: 66.7 us; the launch traced here: 66.5 us
  Pallas kernels  65.9 us (99%)
    pallas_call x1, Pallas kernels, on_device(): pl.pallas_call(functools.partial(kernel, freq_size, sens_size, plan), out...  65.1 us

profile of v5, /device:TPU:0, one launch (start us, length us, event | category | flops | bytes accessed | tf_op | source)
XLA Modules:
  0.0 66.5 jit_solution(9355476398507815228)
XLA Ops:
  0.6 65.1 %shard_map.86 = (bf16[21,16,420]{2,1,0:T(8,128)(2,1)S(1)}, f32[1,21]{1,0:T(1,128)S(1)}) custom-call(bf16[56,21,2,152]{3,2,1,0:T(2,128)(2,1)} %bitcast.3, bf16[16,152,420]{2,1,0:T(8,128)(2,1)} %samples_in.1, bf16[2,456,420]{2,1,0:T(8,128)(2,1)} %constant.4.clone.forward_in, bf16[8,192,420]{2,1,0:T(8,128)(2,1)} %constant.5.clone.inverse_in, s32[152]{0:T(256)} %slots_in.1, ...), custom_call_target="tpu_custom_call" | custom-call | tf_op jit(solution)/shard_map/pallas_call | solution.py:534
  65.7 0.8 %shard_map.87 = (bf16[21,16,420]{2,1,0:T(8,128)(2,1)}, f32[1,21]{1,0:T(1,128)}) custom-call(bf16[21,16,420]{2,1,0:T(8,128)(2,1)S(1)} %get-tuple-element.6.outlook_in, f32[1,21]{1,0:T(1,128)S(1)} %get-tuple-element.7.spread_in), custom_call_target="tpu_custom_call" | custom-call | tf_op jit(solution)/shard_map/pallas_call | solution.py:581

commit v6 on v5

--- a/solution.py
+++ b/solution.py
@@ -36,7 +36,7 @@
         self.pad = -(-self.m // 16) * 16
         self.rows = [sum(map(self.height, part)) for part in self.parts]
         self.held_rows = -(-max(self.rows) // 16) * 16
-        ends = sorted({0, -(-self.m * 3 // 10), self.m - self.m // 5, self.m})
+        ends = sorted({0, self.m * 6 // 10, self.m})
         self.halves = halves = len(ends) - 1
         self.spans = list(zip(ends[:-1], ends[1:]))
         self.pieces = [(d, h) for h in range(halves) for d in range(2)]
@@ -128,7 +128,7 @@
             (forward_in, forward), (samples_in, samples), (inverse_in, inverse),
         ))
     ]
-    for load in sum(tile_loads, []) + loads:
+    for load in sum(tile_loads, []):
         load.start()
 
     right, left = along(1), along(-1)
@@ -192,6 +192,9 @@
         if at == 0:
             pl.semaphore_wait(barrier, 2 + sens_size - 1)
         ring_copy(0, piece, False).start()
+        if at == 1:
+            for load in loads:
+                load.start()
 
     for load in loads[:3]:
         load.wait()

time: 66.7 us -> 66.7 us (level)
  no operation moved by 1% of the time
where the time goes in v6:
time: 66.7 us; the launch traced here: 66.5 us
  Pallas kernels  65.9 us (99%)
    pallas_call x1, Pallas kernels, on_device(): pl.pallas_call(functools.partial(kernel, freq_size, sens_size, plan), out...  65.1 us

profile of v6, /device:TPU:0, one launch (start us, length us, event | category | flops | bytes accessed | tf_op | source)
XLA Modules:
  0.0 66.5 jit_solution(15686420543897223564)
XLA Ops:
  0.6 65.1 %shard_map.86 = (bf16[21,16,420]{2,1,0:T(8,128)(2,1)S(1)}, f32[1,21]{1,0:T(1,128)S(1)}) custom-call(bf16[56,21,2,152]{3,2,1,0:T(2,128)(2,1)} %bitcast.3, bf16[16,152,420]{2,1,0:T(8,128)(2,1)} %samples_in.1, bf16[2,456,420]{2,1,0:T(8,128)(2,1)} %constant.4.clone.forward_in, bf16[8,192,420]{2,1,0:T(8,128)(2,1)} %constant.5.clone.inverse_in, s32[152]{0:T(256)} %slots_in.1, ...), custom_call_target="tpu_custom_call" | custom-call | tf_op jit(solution)/shard_map/pallas_call | solution.py:537
  65.8 0.8 %shard_map.87 = (bf16[21,16,420]{2,1,0:T(8,128)(2,1)}, f32[1,21]{1,0:T(1,128)}) custom-call(bf16[21,16,420]{2,1,0:T(8,128)(2,1)S(1)} %get-tuple-element.6.outlook_in, f32[1,21]{1,0:T(1,128)S(1)} %get-tuple-element.7.spread_in), custom_call_target="tpu_custom_call" | custom-call | tf_op jit(solution)/shard_map/pallas_call | solution.py:584
